TPU v7x, 32 devices: a whole 2x2x4 slice. The times are simulated.
32 devices in a mesh: rows: 8 (over z, y), dp: 4 (over x, core).
Axes of the slice: x: 2, y: 2, z: 4, core: 2. Of those that a mesh axis runs over, the one named last changes fastest.
Arguments:
- weights: float32 [6144, 4096], P(('rows', 'dp'))
- moment: float32 [6144, 4096], P(('rows', 'dp'))
- second: float32 [6144, 4096], P(('rows', 'dp')), may hold values from 0.01 to 1
- tile_rows: bfloat16 [2048, 4096], P(('rows', 'dp')), may hold values from -6 to 6
- row_index: int32 [2048], P(('rows', 'dp')), may hold values from 0 to 191
- bucket_count: int32 [1024], P(('rows', 'dp')), may hold values from 1 to 2, as said below
Outputs:
- new_weights: float32 [6144, 4096], P(('rows', 'dp'))
- new_moment: float32 [6144, 4096], P(('rows', 'dp'))
- new_second: float32 [6144, 4096], P(('rows', 'dp'))
Inputs may be any that keep to these rules, and one draw needn't show every extreme that they name: `bucket_count`: at least one slot of every sender and owner is live; in every draw some owner receives 2 live slots from every sender. `row_index`: rows may repeat within and across senders.
All inputs are finite; a program needn't handle non-finite values.
Results may differ from a plain program's by a relative error of at most 0.0003.
Values may be sent and summed in bfloat16 or wider, within the bound.
A program may use at most 64 MiB of HBM per device.

v0:
```python
import functools

import jax
import jax.numpy as jnp
from jax import lax
from jax.experimental import pallas as pl
from jax.experimental.pallas import tpu as pltpu
from jax.sharding import PartitionSpec as P

beta_one = 0.9
beta_two = 0.999
epsilon = 1e-06
decay = 0.01
rate = 0.1

AXES = ("rows", "dp")
LANES = 128
CHUNKS = 8


def exchange(
    n, fast, weights, moment, second, tiles, index, count,
    weight_out, moment_out, second_out, update_out, scale_out,
    staged, landed, index_all, count_all, parts, picker,
    load_sem, stage_sem, own_sem, tile_send, tile_recv, small_send, small_recv, part_send, part_recv,
):
    me = lax.axis_index("rows") * fast + lax.axis_index("dp")
    rows_here, width = weights.shape
    groups = width // LANES
    slots = index.shape[-1]
    capacity = slots // n
    per = groups // CHUNKS
    pack = tiles.shape[2]

    loads = [
        pltpu.make_async_copy(weights, weight_out, load_sem.at[0]),
        pltpu.make_async_copy(moment, moment_out, load_sem.at[1]),
        pltpu.make_async_copy(second, second_out, load_sem.at[2]),
    ]
    barrier = pltpu.get_barrier_semaphore()

    def place(device):
        return {"rows": device // fast, "dp": lax.rem(device, fast)}

    def peer_of(step):
        return lax.rem(me + 1 + step, n)

    @pl.loop(0, n - 1)
    def _(step):
        pl.semaphore_signal(
            barrier, inc=1, device_id=place(peer_of(step)),
            device_id_type=pl.DeviceIdType.MESH,
        )

    stage = [
        pltpu.make_async_copy(tiles, staged, stage_sem.at[0]),
        pltpu.make_async_copy(index, index_all.at[me], stage_sem.at[1]),
        pltpu.make_async_copy(count, count_all.at[me], stage_sem.at[2]),
    ]
    for copy in stage:
        copy.start()
    own = pltpu.make_async_copy(
        tiles.at[me // pack, :, lax.rem(me, pack)], landed.at[:, me], own_sem
    )
    own.start()
    for load in loads:
        load.start()
    for copy in stage:
        copy.wait()
    pl.semaphore_wait(barrier, n - 1)

    for q in range(CHUNKS):
        span = pl.ds(q * per, per)

        @pl.loop(0, n - 1)
        def _(step):
            peer = peer_of(step)
            pltpu.make_async_remote_copy(
                src_ref=staged.at[peer // pack, span, lax.rem(peer, pack)],
                dst_ref=landed.at[span, me],
                send_sem=tile_send.at[q], recv_sem=tile_recv.at[q],
                device_id=place(peer), device_id_type=pl.DeviceIdType.MESH,
            ).start()

        if q == 0:

            @pl.loop(0, n - 1)
            def _(step):
                peer = peer_of(step)
                for ref, k in ((index_all, 0), (count_all, 1)):
                    pltpu.make_async_remote_copy(
                        src_ref=ref.at[me], dst_ref=ref.at[me],
                        send_sem=small_send.at[k], recv_sem=small_recv.at[k],
                        device_id=place(peer), device_id_type=pl.DeviceIdType.MESH,
                    ).start()

    loads[0].wait()

    def weight_step(g, total):
        w = weight_out[:, pl.ds(pl.multiple_of(g * LANES, LANES), LANES)]
        return total + jnp.sum((w * w).reshape(rows_here // 8, 8, LANES), axis=0)

    zero = jnp.zeros((8, LANES), jnp.float32)
    weight_sum = lax.fori_loop(0, groups, weight_step, zero, unroll=4)

    few = pl.ds(0, n - 1)
    for k, ref in enumerate((index_all, count_all)):
        pltpu.make_async_copy(ref.at[few], ref.at[few], small_recv.at[k]).wait()
    index_rows = index_all[:, 0, :]
    count_rows = count_all[:, 0, :]
    lane = lax.broadcasted_iota(jnp.int32, (n, slots), 1)
    sender = lax.broadcasted_iota(jnp.int32, (n, slots), 0)
    owner = lax.broadcasted_iota(jnp.int32, (n, n), 1)
    live = jnp.sum(jnp.where(owner == me, count_rows, 0), axis=1, keepdims=True)
    spread = jnp.zeros((n, slots), jnp.int32)
    for c in range(capacity):
        mine = jnp.sum(
            jnp.where(lane == me * capacity + c, index_rows, 0), axis=1, keepdims=True
        )
        mine = jnp.where(live > c, mine, -1)
        spread = spread + jnp.where(lane == sender * capacity + c, mine, 0)
    target = jnp.sum(spread, axis=0, keepdims=True)
    row = lax.broadcasted_iota(jnp.int32, (rows_here, slots), 0)
    picker[...] = jnp.where(row == target, 1.0, 0.0).astype(jnp.bfloat16)

    loads[1].wait()
    loads[2].wait()
    own.wait()
    update_sum = zero
    for q in range(CHUNKS):
        span = pl.ds(q * per, per)
        piece = landed.at[span, few]
        pltpu.make_async_copy(piece, piece, tile_recv.at[q]).wait()

        def step(g, total):
            cols = pl.ds(pl.multiple_of(g * LANES, LANES), LANES)
            block = landed[g].reshape(slots, LANES)
            gradient = jnp.dot(
                picker[...], block, preferred_element_type=jnp.float32
            )
            new_moment = beta_one * moment_out[:, cols] + (1.0 - beta_one) * gradient
            new_second = (
                beta_two * second_out[:, cols] + (1.0 - beta_two) * gradient * gradient
            )
            update = (
                new_moment / (jnp.sqrt(new_second) + epsilon)
                + decay * weight_out[:, cols]
            )
            moment_out[:, cols] = new_moment
            second_out[:, cols] = new_second
            update_out[:, cols] = update
            return total + jnp.sum(
                (update * update).reshape(rows_here // 8, 8, LANES), axis=0
            )

        update_sum = lax.fori_loop(q * per, (q + 1) * per, step, update_sum, unroll=4)

    parts[me, 0:1, :] = jnp.sum(weight_sum, axis=0, keepdims=True)
    parts[me, 1:2, :] = jnp.sum(update_sum, axis=0, keepdims=True)

    @pl.loop(0, n - 1)
    def _(step):
        pltpu.make_async_remote_copy(
            src_ref=parts.at[me], dst_ref=parts.at[me],
            send_sem=part_send, recv_sem=part_recv,
            device_id=place(peer_of(step)), device_id_type=pl.DeviceIdType.MESH,
        ).start()

    for k, ref in enumerate((index_all, count_all)):
        pltpu.make_async_copy(ref.at[few], ref.at[few], small_send.at[k]).wait()
    for q in range(CHUNKS):
        piece = landed.at[pl.ds(q * per, per), few]
        pltpu.make_async_copy(piece, piece, tile_send.at[q]).wait()
    pltpu.make_async_copy(parts.at[few], parts.at[few], part_recv).wait()
    pltpu.make_async_copy(parts.at[few], parts.at[few], part_send).wait()

    def total(k):
        lanes = jnp.sum(parts[:, k, :], axis=0, keepdims=True)
        return jnp.sum(lanes, axis=1, keepdims=True)

    trust = jnp.sqrt(total(0)) / jnp.sqrt(total(1) + 1e-06)
    scale_out[...] = jnp.broadcast_to(rate * trust, scale_out.shape)


def finish(
    weight, moment, second, update, scale,
    weight_out, moment_out, second_out, fresh, sem, piece_sem,
):
    copies = [
        pltpu.make_async_copy(moment, moment_out, sem.at[0]),
        pltpu.make_async_copy(second, second_out, sem.at[1]),
    ]
    for copy in copies:
        copy.start()
    rows_here = weight.shape[0]
    pieces = piece_sem.shape[0]
    height = rows_here // pieces
    factor = scale[0:1, 0:1]
    out = []
    for p in range(pieces):
        span = pl.ds(p * height, height)
        fresh[span, :] = weight[span, :] - factor * update[span, :]
        copy = pltpu.make_async_copy(
            fresh.at[span], weight_out.at[span], piece_sem.at[p]
        )
        copy.start()
        out.append(copy)
    for copy in copies + out:
        copy.wait()


def local(n, fast, weights, moment, second, tile_rows, row_index, bucket_count):
    rows_here, width = weights.shape
    slots = row_index.shape[0]
    capacity = slots // n
    groups = width // LANES
    pack = 8 // capacity
    tiles = tile_rows.reshape(n // pack, pack, capacity, groups, LANES)
    tiles = tiles.transpose(0, 3, 1, 2, 4)
    table = (rows_here, width)
    anywhere = pl.BlockSpec(memory_space=pl.ANY)
    outside = pl.BlockSpec(memory_space=pltpu.HBM)
    inside = pl.BlockSpec(memory_space=pltpu.VMEM)
    f32 = jnp.float32
    held = pltpu.VMEM(table, f32)
    weight_v, moment_v, second_v, update_v, scale = pl.pallas_call(
        functools.partial(exchange, n, fast),
        out_shape=[jax.ShapeDtypeStruct(table, f32)] * 4
        + [jax.ShapeDtypeStruct((8, LANES), f32)],
        in_specs=[outside] * 6,
        out_specs=[inside] * 5,
        scratch_shapes=[
            pltpu.VMEM(tiles.shape, jnp.bfloat16),
            pltpu.VMEM((groups, n, capacity, LANES), jnp.bfloat16),
            pltpu.VMEM((n, 1, slots), jnp.int32),
            pltpu.VMEM((n, 1, n), jnp.int32),
            pltpu.VMEM((n, 2, LANES), f32),
            pltpu.VMEM((rows_here, slots), jnp.bfloat16),
            pltpu.SemaphoreType.DMA((3,)),
            pltpu.SemaphoreType.DMA((3,)),
            pltpu.SemaphoreType.DMA,
            pltpu.SemaphoreType.DMA((CHUNKS,)),
            pltpu.SemaphoreType.DMA((CHUNKS,)),
            pltpu.SemaphoreType.DMA((2,)),
            pltpu.SemaphoreType.DMA((2,)),
            pltpu.SemaphoreType.DMA,
            pltpu.SemaphoreType.DMA,
        ],
        compiler_params=pltpu.CompilerParams(
            collective_id=0, has_side_effects=True, vmem_limit_bytes=24 * 1024 * 1024
        ),
        name="exchange",
    )(*(
        pltpu.with_memory_space_constraint(x, pltpu.HBM)
        for x in (
            weights, moment, second, tiles,
            row_index.reshape(1, slots), bucket_count.reshape(1, n),
        )
    ))
    pieces = 6
    return tuple(pl.pallas_call(
        finish,
        out_shape=[jax.ShapeDtypeStruct(table, f32)] * 3,
        in_specs=[inside] * 5,
        out_specs=[anywhere] * 3,
        scratch_shapes=[
            held,
            pltpu.SemaphoreType.DMA((2,)),
            pltpu.SemaphoreType.DMA((pieces,)),
        ],
        compiler_params=pltpu.CompilerParams(vmem_limit_bytes=24 * 1024 * 1024),
        name="finish",
    )(weight_v, moment_v, second_v, update_v, scale))


def solution(mesh):
    n = mesh.shape["rows"] * mesh.shape["dp"]
    rows, flat = P(AXES, None), P(AXES)
    return jax.shard_map(
        functools.partial(local, n, mesh.shape["dp"]),
        mesh=mesh,
        in_specs=(rows, rows, rows, rows, flat, flat),
        out_specs=(rows, rows, rows),
        check_vma=False,
    )
```

profile of v0, /device:TPU:0, one launch (start us, length us, event | category | flops | bytes accessed | tf_op | source)
XLA Modules:
  0.0 31.6 jit_solution(10642764146603261687)
XLA Ops:
  0.6 27.2 %exchange.1 = (f32[192,4096]{1,0:T(8,128)S(1)}, f32[192,4096]{1,0:T(8,128)S(1)}, f32[192,4096]{1,0:T(8,128)S(1)}, f32[192,4096]{1,0:T(8,128)S(1)}, f32[8,128]{1,0:T(8,128)S(1)}) custom-call(f32[192,4096]{1,0:T(8,128)} %weights.1, f32[192,4096]{1,0:T(8,128)} %moment.1, f32[192,4096]{1,0:T(8,128)} %second.1, bf16[8,32,4,2,128]{4,3,2,1,0:T(2,128)(2,1)} %bitcast.5, ...), custom_call_target="tpu_custom_call" | custom-call | tf_op jit(solution)/shard_map/exchange/pallas_call | solution.py:226
  27.9 3.7 %finish.1 = (f32[192,4096]{1,0:T(8,128)}, f32[192,4096]{1,0:T(8,128)}, f32[192,4096]{1,0:T(8,128)}) custom-call(f32[192,4096]{1,0:T(8,128)S(1)} %get-tuple-element.8.weight, f32[192,4096]{1,0:T(8,128)S(1)} %get-tuple-element.9.moment, f32[192,4096]{1,0:T(8,128)S(1)} %get-tuple-element.10.second, f32[192,4096]{1,0:T(8,128)S(1)} %get-tuple-element.11.update, ...), custom_call_target="tpu_custom_call" | custom-call | tf_op jit(solution)/shard_map/finish/pallas_call | solution.py:261
where the time goes:
time: 31.7 us; the launch traced here: 31.6 us
  Pallas kernels  30.9 us (97%)
  between operations  0.64 us (2%)
    pallas_call x1, Pallas kernels, local(): pl.pallas_call(functools.partial(exchange, n, fast), out_shape=[jax.Shape...  27.2 us
    pallas_call x1, Pallas kernels, local(): pl.pallas_call(finish, out_shape=[jax.ShapeDtypeStruct(table, f32)] * 3,...  3.73 us

commit v1 on v0

v1 whole, which is shorter than its diff:
```python
import functools

import jax
import jax.numpy as jnp
from jax import lax
from jax.experimental import pallas as pl
from jax.experimental.pallas import tpu as pltpu
from jax.sharding import PartitionSpec as P

beta_one = 0.9
beta_two = 0.999
epsilon = 1e-06
decay = 0.01
rate = 0.1

AXES = ("rows", "dp")
LANES = 128


def factors(rows, dp):
    lo = max(d for d in range(1, rows + 1) if rows % d == 0 and d * d <= rows)
    core = 2 if dp % 2 == 0 else 1
    return rows // lo, lo, dp // core, core


def pieces_of(groups):
    big = max(groups // 8, 1)
    sizes = [big] * (groups // big)
    while sizes[-1] > 1:
        last = sizes.pop()
        sizes += [last - last // 2, last // 2]
    return sizes


def exchange(
    grid, weights, moment, second, tiles, index, count,
    weight_out, moment_out, second_out, update_out, scale_out,
    staged, landed, index_all, count_all, parts, picker,
    load_sem, stage_sem, own_sem, ready, near_send, near_recv, tile_send, tile_recv,
    line_send, line_recv, plane_send, plane_recv, part_send, part_recv,
):
    Z, L, X, C = grid
    n = Z * L * X * C
    fast = X * C
    columns = L * X * C
    row_id, dp_id = lax.axis_index("rows"), lax.axis_index("dp")
    me = row_id * fast + dp_id
    hi, lo = row_id // L, lax.rem(row_id, L)
    x, core = dp_id // C, lax.rem(dp_id, C)
    column = lo * fast + dp_id
    rows_here, width = weights.shape
    groups = width // LANES
    slots = index.shape[-1]
    capacity = slots // n
    pack = tiles.shape[2]
    sizes = pieces_of(groups)

    half = Z // 2 if Z % 2 == 0 else 0
    if half:
        side = hi // half
        inside = hi - side * half
        line = [side * k + (1 - side) * (Z - 1 - k) for k in range(half)]
        line += [side * half + lax.rem(inside + j, half) for j in range(1, half)]
    else:
        line = [lax.rem(hi + j, Z) for j in range(1, Z)]
    los = [lo] + [lax.rem(lo + j, L) for j in range(1, L)]
    xs = [x] + [lax.rem(x + j, X) for j in range(1, X)]
    cores = [core] + [lax.rem(core + j, C) for j in range(1, C)]

    def spot(h, a, b, c):
        r, d = h * L + a, b * C + c
        return {"rows": r, "dp": d}, r * fast + d

    others = [
        (a, b, c)
        for j, a in list(enumerate(los))[::-1]
        for k, b in list(enumerate(xs))[::-1]
        if j or k
        for c in cores
    ]
    line_peers = [spot(h, lo, x, core) for h in line]
    plane_peers = [spot(hi, a, b, c) for a, b, c in others]
    plane_peers += [spot(hi, lo, x, c) for c in cores[1:]]
    near = [spot(h, lo, x, c) for h in line for c in cores] + plane_peers
    far = [spot(h, a, b, c) for h in line for a, b, c in others]

    def mesh_copy(src, dst, send, recv, where):
        return pltpu.make_async_remote_copy(
            src_ref=src, dst_ref=dst, send_sem=send, recv_sem=recv,
            device_id=where, device_id_type=pl.DeviceIdType.MESH,
        )

    def drain(ref, sem):
        pltpu.make_async_copy(ref, ref, sem).wait()

    stage = [
        pltpu.make_async_copy(tiles, staged, stage_sem.at[0]),
        pltpu.make_async_copy(index, index_all.at[column, hi], stage_sem.at[1]),
        pltpu.make_async_copy(count, count_all.at[column, hi], stage_sem.at[2]),
    ]
    for copy in stage:
        copy.start()
    barrier = pltpu.get_barrier_semaphore()
    for where, _ in near:
        pl.semaphore_signal(
            barrier, inc=1, device_id=where, device_id_type=pl.DeviceIdType.MESH
        )
    own = pltpu.make_async_copy(
        tiles.at[me // pack, :, lax.rem(me, pack)], landed.at[:, me], own_sem
    )
    own.start()
    loads = [
        pltpu.make_async_copy(weights, weight_out, load_sem.at[0]),
        pltpu.make_async_copy(moment, moment_out, load_sem.at[1]),
        pltpu.make_async_copy(second, second_out, load_sem.at[2]),
    ]
    for load in loads:
        load.start()
    for copy in stage:
        copy.wait()
    pl.semaphore_wait(barrier, len(near))

    for where, _ in line_peers:
        pl.semaphore_signal(
            ready, inc=1, device_id=where, device_id_type=pl.DeviceIdType.MESH
        )
    for where, peer in near:
        mesh_copy(
            staged.at[peer // pack, :, lax.rem(peer, pack)], landed.at[:, me],
            near_send, near_recv, where,
        ).start()
    small = (index_all, count_all)
    for k, ref in enumerate(small):
        mine = ref.at[column, hi]
        for where, _ in line_peers:
            mesh_copy(mine, mine, line_send.at[k], line_recv.at[k], where).start()

    if line_peers:
        pl.semaphore_wait(ready, len(line_peers))
    start = 0
    for q, size in enumerate(sizes):
        span = pl.ds(start, size)
        for where, peer in far:
            mesh_copy(
                staged.at[peer // pack, span, lax.rem(peer, pack)],
                landed.at[span, me], tile_send.at[q], tile_recv.at[q], where,
            ).start()
        start += size

    for k, ref in enumerate(small):
        if line_peers:
            drain(ref.at[column, pl.ds(0, Z - 1)], line_recv.at[k])
        block = ref.at[column]
        for where, _ in plane_peers:
            mesh_copy(block, block, plane_send.at[k], plane_recv.at[k], where).start()

    loads[0].wait()

    def weight_step(g, total):
        w = weight_out[:, pl.ds(pl.multiple_of(g * LANES, LANES), LANES)]
        return total + jnp.sum((w * w).reshape(rows_here // 8, 8, LANES), axis=0)

    zero = jnp.zeros((8, LANES), jnp.float32)
    weight_sum = lax.fori_loop(0, groups, weight_step, zero, unroll=4)
    weight_row = jnp.sum(weight_sum, axis=0, keepdims=True)
    weight_row = weight_row + pltpu.roll(weight_row, LANES // 2, 1)

    if plane_peers:
        for k, ref in enumerate(small):
            drain(ref.at[pl.ds(0, columns - 1)], plane_recv.at[k])
    index_rows = jnp.concatenate([index_all[:, h, 0, :] for h in range(Z)], axis=0)
    count_rows = jnp.concatenate([count_all[:, h, 0, :] for h in range(Z)], axis=0)
    lane = lax.broadcasted_iota(jnp.int32, (n, slots), 1)
    order = lax.broadcasted_iota(jnp.int32, (n, slots), 0)
    owner = lax.broadcasted_iota(jnp.int32, (n, n), 1)
    live = jnp.sum(jnp.where(owner == me, count_rows, 0), axis=1, keepdims=True)
    spread = jnp.zeros((n, slots), jnp.int32)
    for c in range(capacity):
        goal = jnp.sum(
            jnp.where(lane == me * capacity + c, index_rows, 0), axis=1, keepdims=True
        )
        goal = jnp.where(live > c, goal, -1)
        spread = spread + jnp.where(lane == order * capacity + c, goal, 0)
    target = jnp.sum(spread, axis=0, keepdims=True)
    row = lax.broadcasted_iota(jnp.int32, (rows_here, slots), 0)
    picker[...] = jnp.where(row == target, 1.0, 0.0).astype(jnp.bfloat16)

    loads[1].wait()
    loads[2].wait()
    own.wait()
    drain(landed.at[:, pl.ds(0, len(near))], near_recv)

    def step(g, total):
        cols = pl.ds(pl.multiple_of(g * LANES, LANES), LANES)
        block = landed[g].reshape(slots, LANES)
        gradient = jnp.dot(picker[...], block, preferred_element_type=jnp.float32)
        new_moment = beta_one * moment_out[:, cols] + (1.0 - beta_one) * gradient
        new_second = (
            beta_two * second_out[:, cols] + (1.0 - beta_two) * gradient * gradient
        )
        update = (
            new_moment / (jnp.sqrt(new_second) + epsilon)
            + decay * weight_out[:, cols]
        )
        moment_out[:, cols] = new_moment
        second_out[:, cols] = new_second
        update_out[:, cols] = update
        return total + jnp.sum(
            (update * update).reshape(rows_here // 8, 8, LANES), axis=0
        )

    update_sum = zero
    start = 0
    for q, size in enumerate(sizes):
        if far:
            drain(landed.at[pl.ds(start, size), pl.ds(0, len(far))], tile_recv.at[q])
        update_sum = lax.fori_loop(start, start + size, step, update_sum, unroll=min(size, 4))
        start += size

    update_row = jnp.sum(update_sum, axis=0, keepdims=True)
    update_row = update_row + pltpu.roll(update_row, LANES // 2, 1)
    left = lax.broadcasted_iota(jnp.int32, (1, LANES), 1) < LANES // 2
    parts[me] = jnp.where(left, update_row, weight_row)
    for where, _ in far + near:
        mesh_copy(parts.at[me], parts.at[me], part_send, part_recv, where).start()

    for k, ref in enumerate(small):
        if line_peers:
            drain(ref.at[column, pl.ds(0, Z - 1)], line_send.at[k])
        if plane_peers:
            drain(ref.at[pl.ds(0, columns - 1)], plane_send.at[k])
    drain(landed.at[:, pl.ds(0, len(near))], near_send)
    start = 0
    for q, size in enumerate(sizes):
        if far:
            drain(landed.at[pl.ds(start, size), pl.ds(0, len(far))], tile_send.at[q])
        start += size
    few = parts.at[pl.ds(0, n - 1)]
    drain(few, part_recv)
    total = jnp.sum(parts[...], axis=0)
    update_sq = jnp.sum(jnp.where(left, total, 0.0), axis=1, keepdims=True)
    weight_sq = jnp.sum(jnp.where(left, 0.0, total), axis=1, keepdims=True)
    trust = jnp.sqrt(weight_sq) / jnp.sqrt(update_sq + 1e-06)
    scale_out[...] = jnp.broadcast_to(rate * trust, scale_out.shape)
    drain(few, part_send)


def finish(
    weight, moment, second, update, scale,
    weight_out, moment_out, second_out, fresh, sem, piece_sem,
):
    copies = [
        pltpu.make_async_copy(moment, moment_out, sem.at[0]),
        pltpu.make_async_copy(second, second_out, sem.at[1]),
    ]
    for copy in copies:
        copy.start()
    rows_here = weight.shape[0]
    pieces = piece_sem.shape[0]
    height = rows_here // pieces
    factor = scale[0:1, 0:1]
    out = []
    for p in range(pieces):
        span = pl.ds(p * height, height)
        fresh[span, :] = weight[span, :] - factor * update[span, :]
        copy = pltpu.make_async_copy(
            fresh.at[span], weight_out.at[span], piece_sem.at[p]
        )
        copy.start()
        out.append(copy)
    for copy in copies + out:
        copy.wait()


def local(grid, weights, moment, second, tile_rows, row_index, bucket_count):
    Z, L, X, C = grid
    n = Z * L * X * C
    rows_here, width = weights.shape
    slots = row_index.shape[0]
    capacity = slots // n
    groups = width // LANES
    pack = 8 // capacity
    tiles = tile_rows.reshape(n // pack, pack, capacity, groups, LANES)
    tiles = tiles.transpose(0, 3, 1, 2, 4)
    table = (rows_here, width)
    anywhere = pl.BlockSpec(memory_space=pl.ANY)
    outside = pl.BlockSpec(memory_space=pltpu.HBM)
    inside = pl.BlockSpec(memory_space=pltpu.VMEM)
    f32 = jnp.float32
    dma = pltpu.SemaphoreType.DMA
    held = pltpu.VMEM(table, f32)
    chunks = len(pieces_of(groups))
    weight_v, moment_v, second_v, update_v, scale = pl.pallas_call(
        functools.partial(exchange, grid),
        out_shape=[jax.ShapeDtypeStruct(table, f32)] * 4
        + [jax.ShapeDtypeStruct((8, LANES), f32)],
        in_specs=[outside] * 6,
        out_specs=[inside] * 5,
        scratch_shapes=[
            pltpu.VMEM(tiles.shape, jnp.bfloat16),
            pltpu.VMEM((groups, n, capacity, LANES), jnp.bfloat16),
            pltpu.VMEM((L * X * C, Z, 1, slots), jnp.int32),
            pltpu.VMEM((L * X * C, Z, 1, n), jnp.int32),
            pltpu.VMEM((n, 1, LANES), f32),
            pltpu.VMEM((rows_here, slots), jnp.bfloat16),
            dma((3,)),
            dma((3,)),
            dma,
            pltpu.SemaphoreType.REGULAR,
            dma, dma,
            dma((chunks,)),
            dma((chunks,)),
            dma((2,)), dma((2,)), dma((2,)), dma((2,)), dma, dma,
        ],
        compiler_params=pltpu.CompilerParams(
            collective_id=0, has_side_effects=True, vmem_limit_bytes=24 * 1024 * 1024
        ),
        name="exchange",
    )(*(
        pltpu.with_memory_space_constraint(x, pltpu.HBM)
        for x in (
            weights, moment, second, tiles,
            row_index.reshape(1, slots), bucket_count.reshape(1, n),
        )
    ))
    pieces = 6
    return tuple(pl.pallas_call(
        finish,
        out_shape=[jax.ShapeDtypeStruct(table, f32)] * 3,
        in_specs=[inside] * 5,
        out_specs=[anywhere] * 3,
        scratch_shapes=[held, dma((2,)), dma((pieces,))],
        compiler_params=pltpu.CompilerParams(vmem_limit_bytes=24 * 1024 * 1024),
        name="finish",
    )(weight_v, moment_v, second_v, update_v, scale))


def solution(mesh):
    grid = factors(mesh.shape["rows"], mesh.shape["dp"])
    rows, flat = P(AXES, None), P(AXES)
    return jax.shard_map(
        functools.partial(local, grid),
        mesh=mesh,
        in_specs=(rows, rows, rows, rows, flat, flat),
        out_specs=(rows, rows, rows),
        check_vma=False,
    )
```

time: 31.7 us -> 29.6 us (0.934)
  Pallas kernels: 30.9 us -> 28.8 us
    pallas_call x1, Pallas kernels: 27.2 us -> 25.1 us  [local(): pl.pallas_call(functools.partial(exchange, grid), out_shape=[jax.ShapeDty...]
where the time goes in v1:
time: 29.6 us; the launch traced here: 29.5 us
  Pallas kernels  28.8 us (97%)
  between operations  0.64 us (2%)
    pallas_call x1, Pallas kernels, local(): pl.pallas_call(functools.partial(exchange, grid), out_shape=[jax.ShapeDty...  25.1 us
    pallas_call x1, Pallas kernels, local(): pl.pallas_call(finish, out_shape=[jax.ShapeDtypeStruct(table, f32)] * 3,...  3.73 us

profile of v1, /device:TPU:0, one launch (start us, length us, event | category | flops | bytes accessed | tf_op | source)
XLA Modules:
  0.0 29.5 jit_solution(14637878397022018596)
XLA Ops:
  0.6 25.1 %exchange.1 = (f32[192,4096]{1,0:T(8,128)S(1)}, f32[192,4096]{1,0:T(8,128)S(1)}, f32[192,4096]{1,0:T(8,128)S(1)}, f32[192,4096]{1,0:T(8,128)S(1)}, f32[8,128]{1,0:T(8,128)S(1)}) custom-call(f32[192,4096]{1,0:T(8,128)} %weights.1, f32[192,4096]{1,0:T(8,128)} %moment.1, f32[192,4096]{1,0:T(8,128)} %second.1, bf16[8,32,4,2,128]{4,3,2,1,0:T(2,128)(2,1)} %bitcast.5, ...), custom_call_target="tpu_custom_call" | custom-call | tf_op jit(solution)/shard_map/exchange/pallas_call | solution.py:293
  25.7 3.7 %finish.1 = (f32[192,4096]{1,0:T(8,128)}, f32[192,4096]{1,0:T(8,128)}, f32[192,4096]{1,0:T(8,128)}) custom-call(f32[192,4096]{1,0:T(8,128)S(1)} %get-tuple-element.8.weight, f32[192,4096]{1,0:T(8,128)S(1)} %get-tuple-element.9.moment, f32[192,4096]{1,0:T(8,128)S(1)} %get-tuple-element.10.second, f32[192,4096]{1,0:T(8,128)S(1)} %get-tuple-element.11.update, ...), custom_call_target="tpu_custom_call" | custom-call | tf_op jit(solution)/shard_map/finish/pallas_call | solution.py:327

commit v2 on v1

--- a/solution.py
+++ b/solution.py
@@ -26,17 +26,16 @@
 def pieces_of(groups):
     big = max(groups // 8, 1)
     sizes = [big] * (groups // big)
-    while sizes[-1] > 1:
-        last = sizes.pop()
-        sizes += [last - last // 2, last // 2]
+    if big > 1:
+        sizes[-1:] = [big - big // 2, big // 2]
     return sizes
 
 
 def exchange(
     grid, weights, moment, second, tiles, index, count,
-    weight_out, moment_out, second_out, update_out, scale_out,
-    staged, landed, index_all, count_all, parts, picker,
-    load_sem, stage_sem, own_sem, ready, near_send, near_recv, tile_send, tile_recv,
+    weight_out, moment_out, second_out, update_out, sums_out,
+    staged, landed, index_all, count_all, parts, picker, moment_in, second_in, decayed,
+    load_sem, stage_sem, own_sem, ready, tile_send, near_recv, far_recv, chunk_recv,
     line_send, line_recv, plane_send, plane_recv, part_send, part_recv,
 ):
     Z, L, X, C = grid
@@ -82,7 +81,8 @@
     plane_peers = [spot(hi, a, b, c) for a, b, c in others]
     plane_peers += [spot(hi, lo, x, c) for c in cores[1:]]
     near = [spot(h, lo, x, c) for h in line for c in cores] + plane_peers
-    far = [spot(h, a, b, c) for h in line for a, b, c in others]
+    cross = [spot(h, a, b, c) for h in line[:half] for a, b, c in others]
+    beside = [spot(h, a, b, c) for h in line[half:] for a, b, c in others]
 
     def mesh_copy(src, dst, send, recv, where):
         return pltpu.make_async_remote_copy(
@@ -92,6 +92,14 @@
 
     def drain(ref, sem):
         pltpu.make_async_copy(ref, ref, sem).wait()
+
+    def send_rows(peers, start, size, recv):
+        span = pl.ds(start, size)
+        for where, peer in peers:
+            mesh_copy(
+                staged.at[peer // pack, span, lax.rem(peer, pack)],
+                landed.at[span, me], tile_send, recv, where,
+            ).start()
 
     stage = [
         pltpu.make_async_copy(tiles, staged, stage_sem.at[0]),
@@ -111,8 +119,8 @@
     own.start()
     loads = [
         pltpu.make_async_copy(weights, weight_out, load_sem.at[0]),
-        pltpu.make_async_copy(moment, moment_out, load_sem.at[1]),
-        pltpu.make_async_copy(second, second_out, load_sem.at[2]),
+        pltpu.make_async_copy(moment, moment_in, load_sem.at[1]),
+        pltpu.make_async_copy(second, second_in, load_sem.at[2]),
     ]
     for load in loads:
         load.start()
@@ -124,46 +132,68 @@
         pl.semaphore_signal(
             ready, inc=1, device_id=where, device_id_type=pl.DeviceIdType.MESH
         )
-    for where, peer in near:
-        mesh_copy(
-            staged.at[peer // pack, :, lax.rem(peer, pack)], landed.at[:, me],
-            near_send, near_recv, where,
-        ).start()
     small = (index_all, count_all)
     for k, ref in enumerate(small):
         mine = ref.at[column, hi]
         for where, _ in line_peers:
             mesh_copy(mine, mine, line_send.at[k], line_recv.at[k], where).start()
+    send_rows(near, 0, groups, near_recv)
 
     if line_peers:
         pl.semaphore_wait(ready, len(line_peers))
-    start = 0
-    for q, size in enumerate(sizes):
-        span = pl.ds(start, size)
-        for where, peer in far:
-            mesh_copy(
-                staged.at[peer // pack, span, lax.rem(peer, pack)],
-                landed.at[span, me], tile_send.at[q], tile_recv.at[q], where,
-            ).start()
-        start += size
-
+    end = (hi == 0) | (hi == Z - 1)
+    inner = jnp.logical_not(end)
+    aside = len(others)
+
+    def send_chunks(peers, some):
+        for q in some:
+            send_rows(peers, sum(sizes[:q]), sizes[q], chunk_recv.at[q])
+
+    chunks = range(len(sizes))
+    soon = len(sizes) // 2
+
+    if half:
+        pl.when(end)(lambda: send_rows(cross, 0, groups, far_recv))
+        if half > 1:
+            @pl.when(inner)
+            def _():
+                send_chunks(cross, chunks[:soon])
+                send_rows(beside, 0, groups, far_recv)
+
+    else:
+        send_rows(beside, 0, groups, far_recv)
     for k, ref in enumerate(small):
         if line_peers:
             drain(ref.at[column, pl.ds(0, Z - 1)], line_recv.at[k])
         block = ref.at[column]
         for where, _ in plane_peers:
             mesh_copy(block, block, plane_send.at[k], plane_recv.at[k], where).start()
+    if half > 1:
+        pl.when(end)(lambda: send_chunks(beside, chunks))
+        pl.when(inner)(lambda: send_chunks(cross, chunks[soon:]))
 
     loads[0].wait()
 
+    def columns_of(g):
+        return pl.ds(pl.multiple_of(g * LANES, LANES), LANES)
+
     def weight_step(g, total):
-        w = weight_out[:, pl.ds(pl.multiple_of(g * LANES, LANES), LANES)]
+        w = weight_out[:, columns_of(g)]
+        decayed[:, columns_of(g)] = decay * w
         return total + jnp.sum((w * w).reshape(rows_here // 8, 8, LANES), axis=0)
 
     zero = jnp.zeros((8, LANES), jnp.float32)
     weight_sum = lax.fori_loop(0, groups, weight_step, zero, unroll=4)
     weight_row = jnp.sum(weight_sum, axis=0, keepdims=True)
     weight_row = weight_row + pltpu.roll(weight_row, LANES // 2, 1)
+
+    loads[1].wait()
+    loads[2].wait()
+
+    @pl.loop(0, groups, unroll=4)
+    def _(g):
+        moment_in[:, columns_of(g)] = beta_one * moment_in[:, columns_of(g)]
+        second_in[:, columns_of(g)] = beta_two * second_in[:, columns_of(g)]
 
     if plane_peers:
         for k, ref in enumerate(small):
@@ -185,23 +215,30 @@
     row = lax.broadcasted_iota(jnp.int32, (rows_here, slots), 0)
     picker[...] = jnp.where(row == target, 1.0, 0.0).astype(jnp.bfloat16)
 
-    loads[1].wait()
-    loads[2].wait()
     own.wait()
     drain(landed.at[:, pl.ds(0, len(near))], near_recv)
 
+    def arrived(start, size, from_end, from_inner, sem):
+        def take(planes):
+            if planes * aside:
+                drain(landed.at[pl.ds(start, size), pl.ds(0, planes * aside)], sem)
+
+        if half > 1:
+            pl.when(end)(lambda: take(from_end))
+            pl.when(inner)(lambda: take(from_inner))
+        else:
+            take(from_end)
+
+    arrived(0, groups, half if half else Z - 1, half - 1, far_recv)
+
     def step(g, total):
-        cols = pl.ds(pl.multiple_of(g * LANES, LANES), LANES)
+        cols = columns_of(g)
         block = landed[g].reshape(slots, LANES)
         gradient = jnp.dot(picker[...], block, preferred_element_type=jnp.float32)
-        new_moment = beta_one * moment_out[:, cols] + (1.0 - beta_one) * gradient
-        new_second = (
-            beta_two * second_out[:, cols] + (1.0 - beta_two) * gradient * gradient
-        )
-        update = (
-            new_moment / (jnp.sqrt(new_second) + epsilon)
-            + decay * weight_out[:, cols]
-        )
+        new_moment = moment_in[:, cols] + (1.0 - beta_one) * gradient
+        new_second = second_in[:, cols] + (1.0 - beta_two) * gradient * gradient
+        root = new_second * lax.rsqrt(new_second)
+        update = new_moment / (root + epsilon) + decayed[:, cols]
         moment_out[:, cols] = new_moment
         second_out[:, cols] = new_second
         update_out[:, cols] = update
@@ -212,16 +249,17 @@
     update_sum = zero
     start = 0
     for q, size in enumerate(sizes):
-        if far:
-            drain(landed.at[pl.ds(start, size), pl.ds(0, len(far))], tile_recv.at[q])
-        update_sum = lax.fori_loop(start, start + size, step, update_sum, unroll=min(size, 4))
+        arrived(start, size, half - 1 if half else 0, half, chunk_recv.at[q])
+        update_sum = lax.fori_loop(
+            start, start + size, step, update_sum, unroll=min(size, 4)
+        )
         start += size
 
     update_row = jnp.sum(update_sum, axis=0, keepdims=True)
     update_row = update_row + pltpu.roll(update_row, LANES // 2, 1)
     left = lax.broadcasted_iota(jnp.int32, (1, LANES), 1) < LANES // 2
     parts[me] = jnp.where(left, update_row, weight_row)
-    for where, _ in far + near:
+    for where, _ in cross + beside + near:
         mesh_copy(parts.at[me], parts.at[me], part_send, part_recv, where).start()
 
     for k, ref in enumerate(small):
@@ -229,24 +267,15 @@
             drain(ref.at[column, pl.ds(0, Z - 1)], line_send.at[k])
         if plane_peers:
             drain(ref.at[pl.ds(0, columns - 1)], plane_send.at[k])
-    drain(landed.at[:, pl.ds(0, len(near))], near_send)
-    start = 0
-    for q, size in enumerate(sizes):
-        if far:
-            drain(landed.at[pl.ds(start, size), pl.ds(0, len(far))], tile_send.at[q])
-        start += size
+    drain(landed.at[:, pl.ds(0, n - 1)], tile_send)
     few = parts.at[pl.ds(0, n - 1)]
     drain(few, part_recv)
-    total = jnp.sum(parts[...], axis=0)
-    update_sq = jnp.sum(jnp.where(left, total, 0.0), axis=1, keepdims=True)
-    weight_sq = jnp.sum(jnp.where(left, 0.0, total), axis=1, keepdims=True)
-    trust = jnp.sqrt(weight_sq) / jnp.sqrt(update_sq + 1e-06)
-    scale_out[...] = jnp.broadcast_to(rate * trust, scale_out.shape)
+    sums_out[...] = jnp.sum(parts[...], axis=0)
     drain(few, part_send)
 
 
 def finish(
-    weight, moment, second, update, scale,
+    weight, moment, second, update, sums,
     weight_out, moment_out, second_out, fresh, sem, piece_sem,
 ):
     copies = [
@@ -258,7 +287,12 @@
     rows_here = weight.shape[0]
     pieces = piece_sem.shape[0]
     height = rows_here // pieces
-    factor = scale[0:1, 0:1]
+    total = sums[...]
+    left = lax.broadcasted_iota(jnp.int32, total.shape, 1) < LANES // 2
+    update_sq = jnp.sum(jnp.where(left, total, 0.0), axis=1, keepdims=True)
+    weight_sq = jnp.sum(jnp.where(left, 0.0, total), axis=1, keepdims=True)
+    trust = jnp.sqrt(weight_sq) / jnp.sqrt(update_sq + 1e-06)
+    factor = rate * trust
     out = []
     for p in range(pieces):
         span = pl.ds(p * height, height)
@@ -289,11 +323,10 @@
     f32 = jnp.float32
     dma = pltpu.SemaphoreType.DMA
     held = pltpu.VMEM(table, f32)
-    chunks = len(pieces_of(groups))
-    weight_v, moment_v, second_v, update_v, scale = pl.pallas_call(
+    weight_v, moment_v, second_v, update_v, sums = pl.pallas_call(
         functools.partial(exchange, grid),
         out_shape=[jax.ShapeDtypeStruct(table, f32)] * 4
-        + [jax.ShapeDtypeStruct((8, LANES), f32)],
+        + [jax.ShapeDtypeStruct((1, LANES), f32)],
         in_specs=[outside] * 6,
         out_specs=[inside] * 5,
         scratch_shapes=[
@@ -303,17 +336,13 @@
             pltpu.VMEM((L * X * C, Z, 1, n), jnp.int32),
             pltpu.VMEM((n, 1, LANES), f32),
             pltpu.VMEM((rows_here, slots), jnp.bfloat16),
-            dma((3,)),
-            dma((3,)),
-            dma,
-            pltpu.SemaphoreType.REGULAR,
-            dma, dma,
-            dma((chunks,)),
-            dma((chunks,)),
+            held, held, held,
+            dma((3,)), dma((3,)), dma, pltpu.SemaphoreType.REGULAR,
+            dma, dma, dma, dma((len(pieces_of(groups)),)),
             dma((2,)), dma((2,)), dma((2,)), dma((2,)), dma, dma,
         ],
         compiler_params=pltpu.CompilerParams(
-            collective_id=0, has_side_effects=True, vmem_limit_bytes=24 * 1024 * 1024
+            collective_id=0, has_side_effects=True, vmem_limit_bytes=36 * 1024 * 1024
         ),
         name="exchange",
     )(*(
@@ -332,7 +361,7 @@
         scratch_shapes=[held, dma((2,)), dma((pieces,))],
         compiler_params=pltpu.CompilerParams(vmem_limit_bytes=24 * 1024 * 1024),
         name="finish",
-    )(weight_v, moment_v, second_v, update_v, scale))
+    )(weight_v, moment_v, second_v, update_v, sums))
 
 
 def solution(mesh):

time: 29.6 us -> 29.1 us (0.983)
  Pallas kernels: 28.8 us -> 28.3 us
    pallas_call x1, Pallas kernels: 25.1 us -> 24.6 us  [local(): pl.pallas_call(functools.partial(exchange, grid), out_shape=[jax.ShapeDty...]
where the time goes in v2:
time: 29.1 us; the launch traced here: 28.9 us
  Pallas kernels  28.3 us (97%)
  between operations  0.64 us (2%)
    pallas_call x1, Pallas kernels, local(): pl.pallas_call(functools.partial(exchange, grid), out_shape=[jax.ShapeDty...  24.6 us
    pallas_call x1, Pallas kernels, local(): pl.pallas_call(finish, out_shape=[jax.ShapeDtypeStruct(table, f32)] * 3,...  3.73 us

profile of v2, /device:TPU:0, one launch (start us, length us, event | category | flops | bytes accessed | tf_op | source)
XLA Modules:
  0.0 28.9 jit_solution(12193276752932371160)
XLA Ops:
  0.6 24.6 %exchange.1 = (f32[192,4096]{1,0:T(8,128)S(1)}, f32[192,4096]{1,0:T(8,128)S(1)}, f32[192,4096]{1,0:T(8,128)S(1)}, f32[192,4096]{1,0:T(8,128)S(1)}, f32[1,128]{1,0:T(1,128)S(1)}) custom-call(f32[192,4096]{1,0:T(8,128)} %weights.1, f32[192,4096]{1,0:T(8,128)} %moment.1, f32[192,4096]{1,0:T(8,128)} %second.1, bf16[8,32,4,2,128]{4,3,2,1,0:T(2,128)(2,1)} %bitcast.5, ...), custom_call_target="tpu_custom_call" | custom-call | tf_op jit(solution)/shard_map/exchange/pallas_call | solution.py:326
  25.2 3.7 %finish.1 = (f32[192,4096]{1,0:T(8,128)}, f32[192,4096]{1,0:T(8,128)}, f32[192,4096]{1,0:T(8,128)}) custom-call(f32[192,4096]{1,0:T(8,128)S(1)} %get-tuple-element.8.weight, f32[192,4096]{1,0:T(8,128)S(1)} %get-tuple-element.9.moment, f32[192,4096]{1,0:T(8,128)S(1)} %get-tuple-element.10.second, f32[192,4096]{1,0:T(8,128)S(1)} %get-tuple-element.11.update, ...), custom_call_target="tpu_custom_call" | custom-call | tf_op jit(solution)/shard_map/finish/pallas_call | solution.py:356

commit v3 on v2

--- a/solution.py
+++ b/solution.py
@@ -24,10 +24,8 @@
 
 
 def pieces_of(groups):
-    big = max(groups // 8, 1)
-    sizes = [big] * (groups // big)
-    if big > 1:
-        sizes[-1:] = [big - big // 2, big // 2]
+    big = groups * 3 // 8
+    sizes = [big, big, groups - 2 * big] if big else [groups]
     return sizes
 
 
@@ -122,10 +120,10 @@
         pltpu.make_async_copy(moment, moment_in, load_sem.at[1]),
         pltpu.make_async_copy(second, second_in, load_sem.at[2]),
     ]
+    for copy in stage:
+        copy.wait()
     for load in loads:
         load.start()
-    for copy in stage:
-        copy.wait()
     pl.semaphore_wait(barrier, len(near))
 
     for where, _ in line_peers:
@@ -145,20 +143,14 @@
     inner = jnp.logical_not(end)
     aside = len(others)
 
-    def send_chunks(peers, some):
-        for q in some:
-            send_rows(peers, sum(sizes[:q]), sizes[q], chunk_recv.at[q])
-
-    chunks = range(len(sizes))
-    soon = len(sizes) // 2
+    def send_chunks(peers):
+        for q, size in enumerate(sizes):
+            send_rows(peers, sum(sizes[:q]), size, chunk_recv.at[q])
 
     if half:
         pl.when(end)(lambda: send_rows(cross, 0, groups, far_recv))
         if half > 1:
-            @pl.when(inner)
-            def _():
-                send_chunks(cross, chunks[:soon])
-                send_rows(beside, 0, groups, far_recv)
+            pl.when(inner)(lambda: send_rows(beside + cross[:aside], 0, groups, far_recv))
 
     else:
         send_rows(beside, 0, groups, far_recv)
@@ -169,8 +161,8 @@
         for where, _ in plane_peers:
             mesh_copy(block, block, plane_send.at[k], plane_recv.at[k], where).start()
     if half > 1:
-        pl.when(end)(lambda: send_chunks(beside, chunks))
-        pl.when(inner)(lambda: send_chunks(cross, chunks[soon:]))
+        pl.when(end)(lambda: send_chunks(beside))
+        pl.when(inner)(lambda: send_chunks(cross[aside:]))
 
     loads[0].wait()
 
@@ -229,7 +221,7 @@
         else:
             take(from_end)
 
-    arrived(0, groups, half if half else Z - 1, half - 1, far_recv)
+    arrived(0, groups, 2 * half - 1 if half else Z - 1, half - 1, far_recv)
 
     def step(g, total):
         cols = columns_of(g)
@@ -249,9 +241,9 @@
     update_sum = zero
     start = 0
     for q, size in enumerate(sizes):
-        arrived(start, size, half - 1 if half else 0, half, chunk_recv.at[q])
+        arrived(start, size, 0, half, chunk_recv.at[q])
         update_sum = lax.fori_loop(
-            start, start + size, step, update_sum, unroll=min(size, 4)
+            start, start + size, step, update_sum, unroll=size
         )
         start += size
 

time: 29.1 us -> 28.6 us (0.983)
  Pallas kernels: 28.3 us -> 27.8 us
    pallas_call x1, Pallas kernels: 24.6 us -> 24.1 us  [local(): pl.pallas_call(functools.partial(exchange, grid), out_shape=[jax.ShapeDty...]
where the time goes in v3:
time: 28.6 us; the launch traced here: 28.5 us
  Pallas kernels  27.8 us (97%)
  between operations  0.64 us (2%)
    pallas_call x1, Pallas kernels, local(): pl.pallas_call(functools.partial(exchange, grid), out_shape=[jax.ShapeDty...  24.1 us
    pallas_call x1, Pallas kernels, local(): pl.pallas_call(finish, out_shape=[jax.ShapeDtypeStruct(table, f32)] * 3,...  3.73 us

profile of v3, /device:TPU:0, one launch (start us, length us, event | category | flops | bytes accessed | tf_op | source)
XLA Modules:
  0.0 28.5 jit_solution(17836795609846491211)
XLA Ops:
  0.6 24.1 %exchange.1 = (f32[192,4096]{1,0:T(8,128)S(1)}, f32[192,4096]{1,0:T(8,128)S(1)}, f32[192,4096]{1,0:T(8,128)S(1)}, f32[192,4096]{1,0:T(8,128)S(1)}, f32[1,128]{1,0:T(1,128)S(1)}) custom-call(f32[192,4096]{1,0:T(8,128)} %weights.1, f32[192,4096]{1,0:T(8,128)} %moment.1, f32[192,4096]{1,0:T(8,128)} %second.1, bf16[8,32,4,2,128]{4,3,2,1,0:T(2,128)(2,1)} %bitcast.5, ...), custom_call_target="tpu_custom_call" | custom-call | tf_op jit(solution)/shard_map/exchange/pallas_call | solution.py:318
  24.7 3.7 %finish.1 = (f32[192,4096]{1,0:T(8,128)}, f32[192,4096]{1,0:T(8,128)}, f32[192,4096]{1,0:T(8,128)}) custom-call(f32[192,4096]{1,0:T(8,128)S(1)} %get-tuple-element.8.weight, f32[192,4096]{1,0:T(8,128)S(1)} %get-tuple-element.9.moment, f32[192,4096]{1,0:T(8,128)S(1)} %get-tuple-element.10.second, f32[192,4096]{1,0:T(8,128)S(1)} %get-tuple-element.11.update, ...), custom_call_target="tpu_custom_call" | custom-call | tf_op jit(solution)/shard_map/finish/pallas_call | solution.py:348

commit v4 on v3

--- a/solution.py
+++ b/solution.py
@@ -24,8 +24,9 @@
 
 
 def pieces_of(groups):
-    big = groups * 3 // 8
-    sizes = [big, big, groups - 2 * big] if big else [groups]
+    small = groups // 4
+    half = (groups - small) // 2
+    sizes = [size for size in (small, half, groups - small - half) if size]
     return sizes
 
 
@@ -70,10 +71,10 @@
 
     others = [
         (a, b, c)
+        for c in cores
         for j, a in list(enumerate(los))[::-1]
         for k, b in list(enumerate(xs))[::-1]
         if j or k
-        for c in cores
     ]
     line_peers = [spot(h, lo, x, core) for h in line]
     plane_peers = [spot(hi, a, b, c) for a, b, c in others]

time: 28.6 us -> 28.4 us (level)
  no operation moved by 1% of the time
where the time goes in v4:
time: 28.4 us; the launch traced here: 28.2 us
  Pallas kernels  27.6 us (97%)
  between operations  0.64 us (2%)
    pallas_call x1, Pallas kernels, local(): pl.pallas_call(functools.partial(exchange, grid), out_shape=[jax.ShapeDty...  23.9 us
    pallas_call x1, Pallas kernels, local(): pl.pallas_call(finish, out_shape=[jax.ShapeDtypeStruct(table, f32)] * 3,...  3.73 us

profile of v4, /device:TPU:0, one launch (start us, length us, event | category | flops | bytes accessed | tf_op | source)
XLA Modules:
  0.0 28.2 jit_solution(1893360738771786325)
XLA Ops:
  0.6 23.9 %exchange.1 = (f32[192,4096]{1,0:T(8,128)S(1)}, f32[192,4096]{1,0:T(8,128)S(1)}, f32[192,4096]{1,0:T(8,128)S(1)}, f32[192,4096]{1,0:T(8,128)S(1)}, f32[1,128]{1,0:T(1,128)S(1)}) custom-call(f32[192,4096]{1,0:T(8,128)} %weights.1, f32[192,4096]{1,0:T(8,128)} %moment.1, f32[192,4096]{1,0:T(8,128)} %second.1, bf16[8,32,4,2,128]{4,3,2,1,0:T(2,128)(2,1)} %bitcast.5, ...), custom_call_target="tpu_custom_call" | custom-call | tf_op jit(solution)/shard_map/exchange/pallas_call | solution.py:319
  24.5 3.7 %finish.1 = (f32[192,4096]{1,0:T(8,128)}, f32[192,4096]{1,0:T(8,128)}, f32[192,4096]{1,0:T(8,128)}) custom-call(f32[192,4096]{1,0:T(8,128)S(1)} %get-tuple-element.8.weight, f32[192,4096]{1,0:T(8,128)S(1)} %get-tuple-element.9.moment, f32[192,4096]{1,0:T(8,128)S(1)} %get-tuple-element.10.second, f32[192,4096]{1,0:T(8,128)S(1)} %get-tuple-element.11.update, ...), custom_call_target="tpu_custom_call" | custom-call | tf_op jit(solution)/shard_map/finish/pallas_call | solution.py:349

commit v5 on v4

--- a/solution.py
+++ b/solution.py
@@ -33,7 +33,7 @@
 def exchange(
     grid, weights, moment, second, tiles, index, count,
     weight_out, moment_out, second_out, update_out, sums_out,
-    staged, landed, index_all, count_all, parts, picker, moment_in, second_in, decayed,
+    staged, landed, index_all, count_all, weight_all, parts, picker, moment_in, second_in, decayed,
     load_sem, stage_sem, own_sem, ready, tile_send, near_recv, far_recv, chunk_recv,
     line_send, line_recv, plane_send, plane_recv, part_send, part_recv,
 ):
@@ -178,7 +178,10 @@
     zero = jnp.zeros((8, LANES), jnp.float32)
     weight_sum = lax.fori_loop(0, groups, weight_step, zero, unroll=4)
     weight_row = jnp.sum(weight_sum, axis=0, keepdims=True)
-    weight_row = weight_row + pltpu.roll(weight_row, LANES // 2, 1)
+    weight_all[column, hi] = weight_row
+    mine = weight_all.at[column, hi]
+    for where, _ in line_peers:
+        mesh_copy(mine, mine, line_send.at[2], line_recv.at[2], where).start()
 
     loads[1].wait()
     loads[2].wait()
@@ -224,6 +227,12 @@
 
     arrived(0, groups, 2 * half - 1 if half else Z - 1, half - 1, far_recv)
 
+    if line_peers:
+        drain(weight_all.at[column, pl.ds(0, Z - 1)], line_recv.at[2])
+    block = weight_all.at[column]
+    for where, _ in plane_peers:
+        mesh_copy(block, block, plane_send.at[2], plane_recv.at[2], where).start()
+
     def step(g, total):
         cols = columns_of(g)
         block = landed[g].reshape(slots, LANES)
@@ -249,21 +258,22 @@
         start += size
 
     update_row = jnp.sum(update_sum, axis=0, keepdims=True)
-    update_row = update_row + pltpu.roll(update_row, LANES // 2, 1)
-    left = lax.broadcasted_iota(jnp.int32, (1, LANES), 1) < LANES // 2
-    parts[me] = jnp.where(left, update_row, weight_row)
+    parts[me] = update_row
     for where, _ in cross + beside + near:
         mesh_copy(parts.at[me], parts.at[me], part_send, part_recv, where).start()
 
-    for k, ref in enumerate(small):
+    for k, ref in enumerate((*small, weight_all)):
         if line_peers:
             drain(ref.at[column, pl.ds(0, Z - 1)], line_send.at[k])
         if plane_peers:
             drain(ref.at[pl.ds(0, columns - 1)], plane_send.at[k])
     drain(landed.at[:, pl.ds(0, n - 1)], tile_send)
+    if plane_peers:
+        drain(weight_all.at[pl.ds(0, columns - 1)], plane_recv.at[2])
+    sums_out[1:2] = jnp.sum(weight_all[...], axis=(0, 1))
     few = parts.at[pl.ds(0, n - 1)]
     drain(few, part_recv)
-    sums_out[...] = jnp.sum(parts[...], axis=0)
+    sums_out[0:1] = jnp.sum(parts[...], axis=0)
     drain(few, part_send)
 
 
@@ -280,10 +290,8 @@
     rows_here = weight.shape[0]
     pieces = piece_sem.shape[0]
     height = rows_here // pieces
-    total = sums[...]
-    left = lax.broadcasted_iota(jnp.int32, total.shape, 1) < LANES // 2
-    update_sq = jnp.sum(jnp.where(left, total, 0.0), axis=1, keepdims=True)
-    weight_sq = jnp.sum(jnp.where(left, 0.0, total), axis=1, keepdims=True)
+    update_sq = jnp.sum(sums[0:1], axis=1, keepdims=True)
+    weight_sq = jnp.sum(sums[1:2], axis=1, keepdims=True)
     trust = jnp.sqrt(weight_sq) / jnp.sqrt(update_sq + 1e-06)
     factor = rate * trust
     out = []
@@ -319,7 +327,7 @@
     weight_v, moment_v, second_v, update_v, sums = pl.pallas_call(
         functools.partial(exchange, grid),
         out_shape=[jax.ShapeDtypeStruct(table, f32)] * 4
-        + [jax.ShapeDtypeStruct((1, LANES), f32)],
+        + [jax.ShapeDtypeStruct((2, LANES), f32)],
         in_specs=[outside] * 6,
         out_specs=[inside] * 5,
         scratch_shapes=[
@@ -327,12 +335,13 @@
             pltpu.VMEM((groups, n, capacity, LANES), jnp.bfloat16),
             pltpu.VMEM((L * X * C, Z, 1, slots), jnp.int32),
             pltpu.VMEM((L * X * C, Z, 1, n), jnp.int32),
+            pltpu.VMEM((L * X * C, Z, 1, LANES), f32),
             pltpu.VMEM((n, 1, LANES), f32),
             pltpu.VMEM((rows_here, slots), jnp.bfloat16),
             held, held, held,
             dma((3,)), dma((3,)), dma, pltpu.SemaphoreType.REGULAR,
             dma, dma, dma, dma((len(pieces_of(groups)),)),
-            dma((2,)), dma((2,)), dma((2,)), dma((2,)), dma, dma,
+            dma((3,)), dma((3,)), dma((3,)), dma((3,)), dma, dma,
         ],
         compiler_params=pltpu.CompilerParams(
             collective_id=0, has_side_effects=True, vmem_limit_bytes=36 * 1024 * 1024

time: 28.4 us -> 30.5 us (1.074)
  Pallas kernels: 27.6 us -> 29.7 us
    pallas_call x1, Pallas kernels: 23.9 us -> 26 us  [local(): pl.pallas_call(functools.partial(exchange, grid), out_shape=[jax.ShapeDty...]
where the time goes in v5:
time: 30.5 us; the launch traced here: 30.3 us
  Pallas kernels  29.7 us (97%)
  between operations  0.64 us (2%)
    pallas_call x1, Pallas kernels, local(): pl.pallas_call(functools.partial(exchange, grid), out_shape=[jax.ShapeDty...  26 us
    pallas_call x1, Pallas kernels, local(): pl.pallas_call(finish, out_shape=[jax.ShapeDtypeStruct(table, f32)] * 3,...  3.73 us

profile of v5, /device:TPU:0, one launch (start us, length us, event | category | flops | bytes accessed | tf_op | source)
XLA Modules:
  0.0 30.3 jit_solution(14140260358516540101)
XLA Ops:
  0.6 26.0 %exchange.1 = (f32[192,4096]{1,0:T(8,128)S(1)}, f32[192,4096]{1,0:T(8,128)S(1)}, f32[192,4096]{1,0:T(8,128)S(1)}, f32[192,4096]{1,0:T(8,128)S(1)}, f32[2,128]{1,0:T(2,128)S(1)}) custom-call(f32[192,4096]{1,0:T(8,128)} %weights.1, f32[192,4096]{1,0:T(8,128)} %moment.1, f32[192,4096]{1,0:T(8,128)} %second.1, bf16[8,32,4,2,128]{4,3,2,1,0:T(2,128)(2,1)} %bitcast.5, ...), custom_call_target="tpu_custom_call" | custom-call | tf_op jit(solution)/shard_map/exchange/pallas_call | solution.py:327
  26.6 3.7 %finish.1 = (f32[192,4096]{1,0:T(8,128)}, f32[192,4096]{1,0:T(8,128)}, f32[192,4096]{1,0:T(8,128)}) custom-call(f32[192,4096]{1,0:T(8,128)S(1)} %get-tuple-element.8.weight, f32[192,4096]{1,0:T(8,128)S(1)} %get-tuple-element.9.moment, f32[192,4096]{1,0:T(8,128)S(1)} %get-tuple-element.10.second, f32[192,4096]{1,0:T(8,128)S(1)} %get-tuple-element.11.update, ...), custom_call_target="tpu_custom_call" | custom-call | tf_op jit(solution)/shard_map/finish/pallas_call | solution.py:358
